TPU v7x, 32 devices: a whole 2x2x4 slice. The times are simulated.
32 devices in a mesh: dp: 4 (over z), row: 4 (over y, x), col: 2 (over core).
Axes of the slice: x: 2, y: 2, z: 4, core: 2. Of those that a mesh axis runs over, the one named last changes fastest.
Arguments:
- layer_input: bfloat16 [8192, 1536], P(('dp', 'row'), 'col'), may hold values from -6 to 6
- gain_attn: float32 [1536], P('col'), may hold values from 0.25 to 1.75
- gain_ffn: float32 [1536], P('col'), may hold values from 0.25 to 1.75
- w_query: bfloat16 [1536, 1536], P('col', 'row'), may hold values from -0.15625 to 0.15625
- w_key: bfloat16 [1536, 768], P('col', 'row'), may hold values from -0.15625 to 0.15625
- w_value: bfloat16 [1536, 768], P('col', 'row'), may hold values from -0.15625 to 0.15625
- w_out: bfloat16 [1536, 1536], P('row', 'col'), may hold values from -1.25 to 1.25
- w_gate: bfloat16 [1536, 4096], P('col', 'row'), may hold values from -0.15625 to 0.15625
- w_up: bfloat16 [1536, 4096], P('col', 'row'), may hold values from -0.15625 to 0.15625
- w_down: bfloat16 [4096, 1536], P('row', 'col'), may hold values from -0.09375 to 0.09375
- cotangent: bfloat16 [8192, 1536], P(('dp', 'row'), 'col'), may hold values from -6 to 6
Outputs:
- layer_output: float32 [8192, 1536], P(('dp', 'row'), 'col')
- grad_input: float32 [8192, 1536], P(('dp', 'row'), 'col')
- grad_gain_attn: float32 [1536], P('col')
- grad_gain_ffn: float32 [1536], P('col')
- grad_query: float32 [1536, 1536], P('col', 'row')
- grad_key: float32 [1536, 768], P('col', 'row')
- grad_value: float32 [1536, 768], P('col', 'row')
- grad_out: float32 [1536, 1536], P('row', 'col')
- grad_gate: float32 [1536, 4096], P('col', 'row')
- grad_up: float32 [1536, 4096], P('col', 'row')
- grad_down: float32 [4096, 1536], P('row', 'col')
All inputs are finite; a program needn't handle non-finite values.
Results may differ from a plain program's by a relative error of at most 0.014.
Values may be sent and summed in bfloat16 or wider, within the bound.
A program may use at most 192 MiB of HBM per device.

v0:
```python
import jax
import jax.numpy as jnp
from jax import lax
from jax.sharding import PartitionSpec as P

D = 1536
HD = 96
LENGTH = 1024
EPS = 1e-05
THETA = 100000.0


def rotate(values, heads, inverse):
    count = values.shape[0]
    half = HD // 2
    pos = (jnp.arange(count) % LENGTH).astype(jnp.float32)
    freq = THETA ** (-jnp.arange(half).astype(jnp.float32) * 2.0 / HD)
    angle = pos[:, None] * freq[None, :]
    cosine = jnp.cos(angle)[:, None, :]
    sine = jnp.sin(angle)[:, None, :]
    shaped = values.reshape(count, heads, HD)
    first = shaped[..., :half]
    second = shaped[..., half:]
    if inverse:
        joined = jnp.concatenate(
            [first * cosine + second * sine, second * cosine - first * sine], -1
        )
    else:
        joined = jnp.concatenate(
            [first * cosine - second * sine, second * cosine + first * sine], -1
        )
    return joined.reshape(count, heads * HD)


def masked_scores(query_block, keys_seq, block_index):
    rows = query_block.shape[0]
    span = keys_seq.shape[0]
    scores = jnp.einsum(
        "qkgd,skd->kgqs", query_block, keys_seq, preferred_element_type=jnp.float32
    ) * HD ** (-0.5)
    qpos = block_index * rows + jnp.arange(rows)
    allowed = jnp.arange(span)[None, :] <= qpos[:, None]
    return jnp.where(allowed[None, None], scores, -1e30)


def attend_forward(queries, keys, values, kv_heads):
    total = queries.shape[0]
    group = queries.shape[1] // (kv_heads * HD)
    block = min(512, LENGTH)
    count = LENGTH // block
    outputs = []
    sums = []
    for seq in range(total // LENGTH):
        start = seq * LENGTH
        keys_seq = keys[start : start + LENGTH].reshape(LENGTH, kv_heads, HD)
        vals_seq = values[start : start + LENGTH].reshape(LENGTH, kv_heads, HD)
        query_seq = queries[start : start + LENGTH].reshape(count, block, kv_heads, group, HD)

        def one_block(pair):
            query_block, index = pair
            scores = masked_scores(query_block, keys_seq, index)
            top = jnp.max(scores, -1, keepdims=True)
            expo = jnp.exp(scores - top)
            total_weight = jnp.sum(expo, -1, keepdims=True)
            probs = (expo / total_weight).astype(jnp.bfloat16)
            mixed = jnp.einsum(
                "kgqs,skd->qkgd", probs, vals_seq, preferred_element_type=jnp.float32
            )
            return (mixed.reshape(block, -1), (top + jnp.log(total_weight))[..., 0])

        mixed, logsum = lax.map(one_block, (query_seq, jnp.arange(count)))
        outputs.append(mixed.reshape(LENGTH, -1))
        sums.append(logsum)
    return (jnp.concatenate(outputs, 0), sums)


def attend_backward(queries, keys, values, grad_mixed, sums, kv_heads):
    total = queries.shape[0]
    group = queries.shape[1] // (kv_heads * HD)
    block = min(512, LENGTH)
    count = LENGTH // block
    scale = HD ** (-0.5)
    grad_q = []
    grad_k = []
    grad_v = []
    for seq in range(total // LENGTH):
        start = seq * LENGTH
        keys_seq = keys[start : start + LENGTH].reshape(LENGTH, kv_heads, HD)
        vals_seq = values[start : start + LENGTH].reshape(LENGTH, kv_heads, HD)
        query_seq = queries[start : start + LENGTH].reshape(count, block, kv_heads, group, HD)
        grad_seq = grad_mixed[start : start + LENGTH].reshape(count, block, kv_heads, group, HD)

        def one_block(carry, quad):
            key_acc, val_acc = carry
            query_block, grad_block, logsum, index = quad
            scores = masked_scores(query_block, keys_seq, index)
            probs = jnp.exp(scores - logsum[..., None])
            grad_probs = jnp.einsum(
                "qkgd,skd->kgqs", grad_block, vals_seq, preferred_element_type=jnp.float32
            )
            inner = jnp.sum(probs * grad_probs, -1, keepdims=True)
            grad_scores = (probs * (grad_probs - inner)).astype(jnp.bfloat16)
            dq_block = (
                jnp.einsum(
                    "kgqs,skd->qkgd", grad_scores, keys_seq, preferred_element_type=jnp.float32
                )
                * scale
            )
            key_acc = (
                key_acc
                + jnp.einsum(
                    "kgqs,qkgd->skd", grad_scores, query_block, preferred_element_type=jnp.float32
                )
                * scale
            )
            val_acc = val_acc + jnp.einsum(
                "kgqs,qkgd->skd",
                probs.astype(jnp.bfloat16),
                grad_block,
                preferred_element_type=jnp.float32,
            )
            return ((key_acc, val_acc), dq_block.reshape(block, -1))

        zero = jnp.zeros((LENGTH, kv_heads, HD), jnp.float32)
        (key_acc, val_acc), dq_seq = lax.scan(
            one_block, (zero, zero), (query_seq, grad_seq, sums[seq], jnp.arange(count))
        )
        grad_q.append(dq_seq.reshape(LENGTH, -1))
        grad_k.append(key_acc.reshape(LENGTH, -1))
        grad_v.append(val_acc.reshape(LENGTH, -1))
    return (jnp.concatenate(grad_q, 0), jnp.concatenate(grad_k, 0), jnp.concatenate(grad_v, 0))


def width_total(values):
    return lax.psum(values, "col")


def gather_tokens(values):
    return lax.all_gather(values, "row", axis=0, tiled=True)


def width_sum(values):
    return lax.psum(values, "col")


def token_sum(source, weight):
    return lax.psum_scatter(
        jnp.einsum("tj,jc->tc", source, weight, preferred_element_type=jnp.float32),
        "row",
        scatter_dimension=0,
        tiled=True,
    )


def on_device(
    layer_input,
    gain_attn,
    gain_ffn,
    w_query,
    w_key,
    w_value,
    w_out,
    w_gate,
    w_up,
    w_down,
    cotangent,
):
    input_f32 = layer_input.astype(jnp.float32)
    q_cols = w_query.shape[1]
    k_cols = w_key.shape[1]
    f_cols = w_gate.shape[1]
    w_in = jnp.concatenate([w_query, w_key, w_value], 1)
    w_gateup = jnp.concatenate([w_gate, w_up], 1)
    rstd1 = lax.rsqrt(width_total(jnp.sum(input_f32 * input_f32, 1)) / D + EPS)[:, None]
    normed_a = (input_f32 * rstd1 * gain_attn).astype(jnp.bfloat16)
    all_a = gather_tokens(normed_a)
    projected = width_sum(jnp.dot(all_a, w_in, preferred_element_type=jnp.float32))
    q_sum = projected[:, :q_cols]
    k_sum = projected[:, q_cols : q_cols + k_cols]
    v_sum = projected[:, q_cols + k_cols :]
    heads_q = q_sum.shape[1] // HD
    heads_k = k_sum.shape[1] // HD
    queries = rotate(q_sum, heads_q, False).astype(jnp.bfloat16)
    keys = rotate(k_sum, heads_k, False).astype(jnp.bfloat16)
    values = v_sum.astype(jnp.bfloat16)
    mixed, sums = attend_forward(queries, keys, values, heads_k)
    own_attn = mixed.astype(jnp.bfloat16)
    hidden = input_f32 + token_sum(own_attn, w_out)
    rstd2 = lax.rsqrt(width_total(jnp.sum(hidden * hidden, 1)) / D + EPS)[:, None]
    normed_f = (hidden * rstd2 * gain_ffn).astype(jnp.bfloat16)
    all_f = gather_tokens(normed_f)
    gateup_part = jnp.dot(all_f, w_gateup, preferred_element_type=jnp.float32)
    gateup = width_sum(gateup_part)
    gate = gateup[:, :f_cols]
    upper = gateup[:, f_cols:]
    sig = 1.0 / (1.0 + jnp.exp(-gate))
    own_middle = (gate * sig * upper).astype(jnp.bfloat16)
    layer_output = hidden + token_sum(own_middle, w_down)
    all_dy = gather_tokens(cotangent)
    gw_down = jnp.einsum("tf,tc->fc", own_middle, all_dy, preferred_element_type=jnp.float32)
    mid_part = jnp.einsum("tc,fc->tf", all_dy, w_down, preferred_element_type=jnp.float32)
    d_mid = width_sum(mid_part)
    d_gate = (d_mid * upper * sig * (1.0 + gate * (1.0 - sig))).astype(jnp.bfloat16)
    d_up = (d_mid * gate * sig).astype(jnp.bfloat16)
    d_gateup = jnp.concatenate([d_gate, d_up], 1)
    gw_gateup = jnp.einsum("tc,tf->cf", all_f, d_gateup, preferred_element_type=jnp.float32)
    d_nf = token_sum(d_gateup, w_gateup.T)
    part_gain_ffn = jnp.sum(d_nf * hidden * rstd2, 0)
    scaled2 = d_nf * gain_ffn
    inner2 = width_total(jnp.sum(scaled2 * hidden, 1))[:, None]
    d_hidden = cotangent.astype(jnp.float32) + rstd2 * scaled2 - hidden * rstd2**3 * inner2 / D
    all_dya = gather_tokens(d_hidden.astype(jnp.bfloat16))
    gw_out = jnp.einsum("tq,tc->qc", own_attn, all_dya, preferred_element_type=jnp.float32)
    attn_part = jnp.einsum("tc,qc->tq", all_dya, w_out, preferred_element_type=jnp.float32)
    d_attn = width_sum(attn_part).astype(jnp.bfloat16)
    dq_rot, dk_rot, dv = attend_backward(queries, keys, values, d_attn, sums, heads_k)
    d_q = rotate(dq_rot, heads_q, True).astype(jnp.bfloat16)
    d_k = rotate(dk_rot, heads_k, True).astype(jnp.bfloat16)
    d_v = dv.astype(jnp.bfloat16)
    d_proj = jnp.concatenate([d_q, d_k, d_v], 1)
    gw_in = jnp.einsum("tc,tj->cj", all_a, d_proj, preferred_element_type=jnp.float32)
    sum_down, sum_gateup, sum_in, sum_out = lax.psum((gw_down, gw_gateup, gw_in, gw_out), "dp")
    d_na = token_sum(d_proj, w_in.T)
    part_gain_attn = jnp.sum(d_na * input_f32 * rstd1, 0)
    scaled1 = d_na * gain_attn
    inner1 = width_total(jnp.sum(scaled1 * input_f32, 1))[:, None]
    grad_input = d_hidden + rstd1 * scaled1 - input_f32 * rstd1**3 * inner1 / D
    gain_a, gain_f = lax.psum((part_gain_attn, part_gain_ffn), ("dp", "row"))
    return (
        layer_output,
        grad_input,
        gain_a,
        gain_f,
        sum_in[:, :q_cols],
        sum_in[:, q_cols : q_cols + k_cols],
        sum_in[:, q_cols + k_cols :],
        sum_out,
        sum_gateup[:, :f_cols],
        sum_gateup[:, f_cols:],
        sum_down,
    )


def solution(mesh):
    return jax.shard_map(
        on_device,
        mesh=mesh,
        in_specs=(
            P(("dp", "row"), "col"),
            P("col"),
            P("col"),
            P("col", "row"),
            P("col", "row"),
            P("col", "row"),
            P("row", "col"),
            P("col", "row"),
            P("col", "row"),
            P("row", "col"),
            P(("dp", "row"), "col"),
        ),
        out_specs=(
            P(("dp", "row"), "col"),
            P(("dp", "row"), "col"),
            P("col"),
            P("col"),
            P("col", "row"),
            P("col", "row"),
            P("col", "row"),
            P("row", "col"),
            P("col", "row"),
            P("col", "row"),
            P("row", "col"),
        ),
        check_vma=False,
    )
```

profile of v0, /device:TPU:0, one launch (start us, length us, event | category | flops | bytes accessed | tf_op | source)
XLA Modules:
  0.0 1411.9 jit_solution(6619210359016683264)
XLA Ops:
  14.7 46.1 %all-gather.5.cloned.1.call-done = bf16[2048,768]{1,0:T(8,128)(2,1)} async-done(((bf16[512,768]{1,0:T(8,128)(2,1)}), bf16[2048,768]{1,0:T(8,128)(2,1)}) %all-gather.5.cloned.1.call-update) | async-done | bytes 3145744 | tf_op jit(solution)/shard_map/all_gather | solution.py:139
  60.9 7.2 fusion.111
  69.6 30.8 %all-reduce.8.cloned.1.call-done = f32[2048,768]{1,0:T(8,128)} async-done(((f32[2048,768]{1,0:T(8,128)}), f32[2048,768]{1,0:T(8,128)}) %all-reduce.8.cloned.1.call-update) | async-done | bytes 6291472 | tf_op jit(solution)/shard_map/psum | solution.py:143
  100.4 3.0 slice.119
  103.5 2.9 copy.41
  106.4 3.8 slice.114
  110.2 3.5 copy.40
  118.5 3.1 convert.47
  126.4 25.8 %while.54 = (s32[]{:T(128)}, bf16[2,512,384]{2,1,0:T(8,128)(2,1)}, f32[2,2,2,512]{3,2,1,0:T(2,128)S(1)}, s32[2]{0:T(128)}, bf16[2,512,2,2,96]{1,4,3,2,0:T(8,128)...) while((s32[]{:T(128)}, bf16[2,512,384]{2,1,0:T(8,128)(2,1)}, ...), condition=%wide.region_6.7_spmd, body=%wide.region_3.6_spmd.sunk | while | flops 830994944 | bytes 30478976 | solution.py:71
  132.8 4.4 fusion.187
  145.7 4.4 fusion.187
  153.0 3.2 reshape.341
  160.8 24.7 %while.55 = (s32[]{:T(128)}, bf16[2,512,384]{2,1,0:T(8,128)(2,1)}, f32[2,2,2,512]{3,2,1,0:T(2,128)}, s32[2]{0:T(128)}, bf16[2,512,2,2,96]{1,4,3,2,0:T(8,128)(2,1...) while((s32[]{:T(128)}, bf16[2,512,384]{2,1,0:T(8,128)(2,1)}, ...), condition=%wide.region_10.11_spmd, body=%wide.region_7.10_spmd.sunk | while | flops 830994944 | bytes 30610104 | solution.py:71
  167.7 3.6 fusion.190
  179.9 3.6 fusion.190
  185.5 6.6 fusion.106
  192.8 70.7 %reduce-scatter.5.cloned.1.call-done = f32[512,768]{1,0:T(8,128)} async-done(((f32[2048,768]{1,0:T(8,128)}), f32[512,768]{1,0:T(8,128)}) %reduce-scatter.5.cloned.1.call-update) | async-done | bytes 1572880 | tf_op jit(solution)/shard_map/reduce_scatter | solution.py:147
  269.0 2.8 constant_dynamic-update-slice_fusion.3
  273.1 36.0 %all-gather.9.cloned.1.call-done = bf16[2048,768]{1,0:T(8,128)(2,1)} async-done(((bf16[512,768]{1,0:T(8,128)(2,1)}), bf16[2048,768]{1,0:T(8,128)(2,1)}) %all-gather.9.cloned.1.call-update) | async-done | bytes 3145744 | tf_op jit(solution)/shard_map/all_gather | solution.py:139
  309.1 7.6 fusion.130
  316.7 38.5 %all-gather.7.cloned.1.call-done = bf16[2048,768]{1,0:T(8,128)(2,1)} async-done(((bf16[512,768]{1,0:T(8,128)(2,1)}), bf16[2048,768]{1,0:T(8,128)(2,1)}) %all-gather.7.cloned.1.call-update) | async-done | bytes 3145744 | tf_op jit(solution)/shard_map/all_gather | solution.py:139
  355.2 12.5 fusion.128
  367.8 82.7 %all-reduce.12.cloned.1.call-done = (f32[2048,2048]{1,0:T(8,128)}, f32[2048,1024]{1,0:T(8,128)}) async-done(((f32[2048,2048]{1,0:T(8,128)}, f32[2048,1024]{1,0:T(8,128)}), (f32[2048,2048]{1,0:T(8,128)}, f32[2048,1024]{1,0:T(8,128)})) %all-reduce.12.cloned.1.call-update) | async-done | bytes 25165840 | tf_op jit(solution)/shard_map/psum | solution.py:143
  450.5 12.9 multiply_convert_fusion.1
  466.6 10.5 fusion.95
  477.1 8.5 fusion.129
  485.7 62.8 %reduce-scatter.9.cloned.1.call-done = f32[512,768]{1,0:T(8,128)} async-done(((f32[2048,768]{1,0:T(8,128)}), f32[512,768]{1,0:T(8,128)}) %reduce-scatter.9.cloned.1.call-update) | async-done | bytes 1572880 | tf_op jit(solution)/shard_map/reduce_scatter | solution.py:147
  553.5 68.1 %reduce-scatter.7.cloned.1.call-done = f32[512,768]{1,0:T(8,128)} async-done(((f32[2048,768]{1,0:T(8,128)}), f32[512,768]{1,0:T(8,128)}) %reduce-scatter.7.cloned.1.call-update) | async-done | bytes 1572880 | tf_op jit(solution)/shard_map/reduce_scatter | solution.py:147
  621.6 4.1 fusion.123
  625.8 43.9 %all-gather.11.cloned.1.call-done = bf16[2048,768]{1,0:T(8,128)(2,1)} async-done(((bf16[512,768]{1,0:T(8,128)(2,1)}), bf16[2048,768]{1,0:T(8,128)(2,1)}) %all-gather.11.cloned.1.call-update) | async-done | bytes 3145744 | tf_op jit(solution)/shard_map/all_gather | solution.py:139
  669.8 5.5 fusion.131
  675.3 12.2 all-reduce.13
  688.8 4.8 reshape.360
  697.6 74.2 %while.56 = (s32[]{:T(128)}, f32[1024,2,96]{0,2,1:T(8,128)}, f32[1024,2,96]{0,2,1:T(8,128)}, f32[2,512,384]{1,0,2:T(2,128)}, bf16[2,512,2,2,96]{1,4,3,2,0:T(8,12...) while((s32[]{:T(128)}, f32[1024,2,96]{0,2,1:T(8,128)}, ...), condition=%wide.region_23.24_spmd.clone, body=%wide.region_21.23_spmd.clone.sunk | while | flops 2046425600 | bytes 131526960 | solution.py:125
  700.6 4.5 fusion.200
  709.8 14.9 %dynamic_update_slice.36 = f32[2,512,384]{1,0,2:T(2,128)} dynamic-update-slice(f32[2,512,384]{1,0,2:T(2,128)} %get-tuple-element.816, f32[1,512,384]{1,0,2:T(1,128)S(1)} %copy.94, s32[]{:T(128)} %get-tuple-element.813, s32[]{:T(128)} %constant.122.clone.1..sunk, s32[]{:T(128)} %constant.122.clone.1..sunk) | dynamic-update-slice | bytes 1572868 | tf_op jit(solution)/shard_map/while/body/jit(dynamic_update_index_in_dim)/dynamic_update_slice | solution.py:71
  724.8 4.0 fusion.202
  728.8 5.7 fusion.203
  737.5 4.5 fusion.200
  746.7 14.9 %dynamic_update_slice.36 = f32[2,512,384]{1,0,2:T(2,128)} dynamic-update-slice(f32[2,512,384]{1,0,2:T(2,128)} %get-tuple-element.816, f32[1,512,384]{1,0,2:T(1,128)S(1)} %copy.94, s32[]{:T(128)} %get-tuple-element.813, s32[]{:T(128)} %constant.122.clone.1..sunk, s32[]{:T(128)} %constant.122.clone.1..sunk) | dynamic-update-slice | bytes 1572868 | tf_op jit(solution)/shard_map/while/body/jit(dynamic_update_index_in_dim)/dynamic_update_slice | solution.py:71
  761.6 4.2 fusion.202
  765.8 5.9 fusion.203
  775.7 4.7 reshape.361
  780.4 3.6 copy.54
  785.5 70.2 %while.57 = (s32[]{:T(128)}, f32[1024,2,96]{0,2,1:T(8,128)S(1)}, f32[1024,2,96]{0,2,1:T(8,128)}, f32[2,512,384]{1,0,2:T(2,128)}, bf16[2,512,2,2,96]{1,4,3,2,0:T(...) while((s32[]{:T(128)}, f32[1024,2,96]{0,2,1:T(8,128)S(1)}, ...), condition=%wide.region_26.27_spmd.clone, body=%wide.region_24.26_spmd.clone.sunk | while | flops 2046425600 | bytes 133099856 | solution.py:125
  788.7 3.2 fusion.213
  796.6 14.9 %dynamic_update_slice.37 = f32[2,512,384]{1,0,2:T(2,128)} dynamic-update-slice(f32[2,512,384]{1,0,2:T(2,128)} %get-tuple-element.777, f32[1,512,384]{1,0,2:T(1,128)S(1)} %copy.95, s32[]{:T(128)} %get-tuple-element.774, s32[]{:T(128)} %constant.122.clone.1..sunk.1, s32[]{:T(128)} %constant.122.clone.1..sunk.1) | dynamic-update-slice | bytes 1572868 | tf_op jit(solution)/shard_map/while/body/jit(dynamic_update_index_in_dim)/dynamic_update_slice | solution.py:71
  811.5 3.2 fusion.215
  814.7 5.8 fusion.216
  823.7 3.2 fusion.213
  831.6 14.9 %dynamic_update_slice.37 = f32[2,512,384]{1,0,2:T(2,128)} dynamic-update-slice(f32[2,512,384]{1,0,2:T(2,128)} %get-tuple-element.777, f32[1,512,384]{1,0,2:T(1,128)S(1)} %copy.95, s32[]{:T(128)} %get-tuple-element.774, s32[]{:T(128)} %constant.122.clone.1..sunk.1, s32[]{:T(128)} %constant.122.clone.1..sunk.1) | dynamic-update-slice | bytes 1572868 | tf_op jit(solution)/shard_map/while/body/jit(dynamic_update_index_in_dim)/dynamic_update_slice | solution.py:71
  846.5 3.2 fusion.215
  849.7 6.0 fusion.216
  855.8 3.7 concatenate.55
  868.3 5.5 fusion.109
  873.9 8.5 fusion.132
  882.4 9.1 fusion.94
  894.5 4.1 fusion.108
  898.7 45.4 %reduce-scatter.11.cloned.1.call-done = f32[512,768]{1,0:T(8,128)} async-done(((f32[2048,768]{1,0:T(8,128)}), f32[512,768]{1,0:T(8,128)}) %reduce-scatter.11.cloned.1.call-update) | async-done | bytes 1572880 | tf_op jit(solution)/shard_map/reduce_scatter | solution.py:147
  948.6 44.6 %all-reduce = (f32[768]{0:T(1024)}, f32[768]{0:T(1024)}) all-reduce(f32[768]{0:T(1024)S(1)} %get-tuple-element.363, f32[768]{0:T(1024)S(1)} %copy-done.59), channel_id=1, replica_groups=mesh['dp'=4,'row'=4,'col'=2] {'dp','row'}, use_global_device_ids=true, to_apply=%region_31.32 | all-reduce | flops 1536 | bytes 12288 | tf_op jit(solution)/shard_map/psum | solution.py:228
  993.2 3.0 fusion.101
  996.3 391.9 %all-reduce.10.cloned.1.call-done = (f32[768,768]{1,0:T(8,128)}, f32[384,768]{1,0:T(8,128)}, f32[768,2048]{1,0:T(8,128)}, f32[1024,768]{1,0:T(8,128)}) async-done(((f32[768,768]{1,0:T(8,128)}, f32[384,768]{1,0:T(8,128)}, f32[768,2048]{1,0:T(8,128)}, f32[1024,768]{1,0:T(8,128)}), (f32[768,768]{1,0:T(8,128)}, f32[384,768]{1,0:T(8,128)}, f32[768,2048]{1,0:T(8,128)}, ...) | async-done | bytes 12976144 | tf_op jit(solution)/shard_map/psum | solution.py:222
  1391.4 6.7 fusion.124
  1401.2 3.8 copy.157
  (301 shorter events, 132.7 us)
Async XLA Ops:
  7.2 301.9 %copy-start = (bf16[1024,768]{1,0:T(8,128)(2,1)S(1)}, bf16[1024,768]{1,0:T(8,128)(2,1)}, u32[]{:S(2)}) copy-start(bf16[1024,768]{1,0:T(8,128)(2,1)} %param.28) | copy-start | bytes 4718596
  7.2 7.2 copy-start.48
  7.2 7.3 copy-start.49
  7.2 53.6 %copy-start.64 = (bf16[768,384]{1,0:T(8,128)(2,1)S(1)}, bf16[768,384]{1,0:T(8,128)(2,1)}, u32[]{:S(2)}) copy-start(bf16[768,384]{1,0:T(8,128)(2,1)} %param.22) | copy-start | bytes 1769476
  7.2 53.6 %all-gather.5.cloned.1.call-start = ((), (), s32[]{:S(2)}) async-start(), calls=%async_computation.4 | async-start | bytes 3932160 | tf_op jit(solution)/shard_map/all_gather | solution.py:139
  14.3 86.1 %all-reduce.8.cloned.1.call-start = ((), (), s32[]{:S(2)}) async-start(), calls=%async_computation.5 | async-start | bytes 12582912 | tf_op jit(solution)/shard_map/psum | solution.py:143
  14.5 53.5 %copy-start.42 = (bf16[768,192]{1,0:T(8,128)(2,1)}, bf16[768,192]{1,0:T(8,128)(2,1)S(1)}, u32[]{:S(2)}) copy-start(bf16[768,192]{1,0:T(8,128)(2,1)S(1)} %copy.38) | copy-start | bytes 884740
  14.7 53.4 %copy-start.44 = (bf16[768,192]{1,0:T(8,128)(2,1)}, bf16[768,192]{1,0:T(8,128)(2,1)S(1)}, u32[]{:S(2)}) copy-start(bf16[768,192]{1,0:T(8,128)(2,1)S(1)} %copy.39) | copy-start | bytes 884740
  68.1 195.4 %reduce-scatter.5.cloned.1.call-start = ((), (), s32[]{:S(2)}) async-start(), calls=%async_computation.6 | async-start | bytes 7864320 | tf_op jit(solution)/shard_map/reduce_scatter | solution.py:147
  69.6 46.7 %copy-start.20 = (f32[2048,48]{0,1:T(8,128)}, f32[2048,48]{0,1:T(8,128)S(1)}, u32[]{:S(2)}) copy-start(f32[2048,48]{0,1:T(8,128)S(1)} %get-tuple-element.477) | copy-start | bytes 1179652
  69.6 46.7 %copy-start.22 = (f32[2048,48]{0,1:T(8,128)}, f32[2048,48]{0,1:T(8,128)S(1)}, u32[]{:S(2)}) copy-start(f32[2048,48]{0,1:T(8,128)S(1)} %get-tuple-element.478) | copy-start | bytes 1179652
  152.1 8.7 copy-start.8
  152.1 8.7 copy-start.50
  167.7 3.7 copy-start.53
  179.8 3.7 copy-start.53
  185.5 6.6 copy-start.6
  185.5 6.6 copy-start.10
  185.5 6.6 copy-start.16
  192.1 75.7 %copy-start.55 = (f32[768]{0:T(1024)S(1)}, f32[768]{0:T(1024)}, u32[]{:S(2)}) copy-start(f32[768]{0:T(1024)} %param.21) | copy-start | bytes 9220
  192.1 116.9 %all-gather.9.cloned.1.call-start = ((), (), s32[]{:S(2)}) async-start(), calls=%async_computation.9 | async-start | bytes 3932160 | tf_op jit(solution)/shard_map/all_gather | solution.py:139
  192.7 162.5 %all-gather.7.cloned.1.call-start = ((), (), s32[]{:S(2)}) async-start(), calls=%async_computation.7 | async-start | bytes 3932160 | tf_op jit(solution)/shard_map/all_gather | solution.py:139
  269.0 181.5 %all-reduce.12.cloned.1.call-start = ((), (), s32[]{:S(2)}) async-start(), calls=%async_computation.14 | async-start | bytes 50331648 | tf_op jit(solution)/shard_map/psum | solution.py:143
  367.7 180.8 %reduce-scatter.9.cloned.1.call-start = ((), (), s32[]{:S(2)}) async-start(), calls=%async_computation.10 | async-start | bytes 7864320 | tf_op jit(solution)/shard_map/reduce_scatter | solution.py:147
  463.4 3.2 copy-start.32
  477.1 144.5 %reduce-scatter.7.cloned.1.call-start = ((), (), s32[]{:S(2)}) async-start(), calls=%async_computation.8 | async-start | bytes 7864320 | tf_op jit(solution)/shard_map/reduce_scatter | solution.py:147
  485.6 184.1 %all-gather.11.cloned.1.call-start = ((), (), s32[]{:S(2)}) async-start(), calls=%async_computation.11 | async-start | bytes 3932160 | tf_op jit(solution)/shard_map/all_gather | solution.py:139
  548.5 73.1 %copy-start.29 = (f32[512,768]{1,0:T(8,128)S(1)}, f32[512,768]{1,0:T(8,128)}, u32[]{:S(2)}) copy-start(f32[512,768]{1,0:T(8,128)} %reduce-scatter.9.cloned.1.call-done) | copy-start | bytes 4718596
  625.8 318.3 %reduce-scatter.11.cloned.1.call-start = ((), (), s32[]{:S(2)}) async-start(), calls=%async_computation.12 | async-start | bytes 7864320 | tf_op jit(solution)/shard_map/reduce_scatter | solution.py:147
  688.8 8.8 copy-start.9
  688.8 8.8 copy-start.13
  688.8 8.8 copy-start.51
  698.9 6.2 copy-start.2
  724.8 4.0 copy-start.27
  735.8 6.2 copy-start.2
  761.6 4.2 copy-start.27
  775.7 9.8 copy-start.7
  775.7 9.8 copy-start.11
  775.7 9.8 copy-start.17
  775.7 9.8 copy-start.54
  785.6 3.1 copy-start.24
  786.9 5.0 copy-start.3
  811.5 3.2 copy-start.25
  814.7 5.8 copy-start.18
  820.5 3.1 copy-start.24
  821.9 5.1 copy-start.3
  846.5 3.2 copy-start.25
  849.7 6.1 copy-start.18
  855.8 6.4 copy-start.21
  855.8 6.4 copy-start.23
  867.8 6.0 copy-start.40
  873.8 514.3 %all-reduce.10.cloned.1.call-start = ((), (), s32[]{:S(2)}) async-start(), calls=%async_computation.13 | async-start | bytes 25952256 | tf_op jit(solution)/shard_map/psum | solution.py:222
  873.9 8.5 copy-start.31
  873.9 8.5 copy-start.33
  873.9 8.5 copy-start.62
  882.4 9.1 copy-start.35
  882.4 9.1 copy-start.36
  882.4 9.1 copy-start.63
  898.6 45.4 %copy-start.15 = (bf16[512,768]{1,0:T(8,128)(2,1)S(1)}, bf16[512,768]{1,0:T(8,128)(2,1)}, u32[]{:S(2)}) copy-start(bf16[512,768]{1,0:T(8,128)(2,1)} %param.19) | copy-start | bytes 2359300
  898.6 45.4 %copy-start.56 = (f32[768]{0:T(1024)S(1)}, f32[768]{0:T(1024)}, u32[]{:S(2)}) copy-start(f32[768]{0:T(1024)} %param.20) | copy-start | bytes 9220
  898.6 45.4 %copy-start.58 = (f32[512]{0:T(512)S(1)}, f32[512]{0:T(512)}, u32[]{:S(2)}) copy-start(f32[512]{0:T(512)} %copy-done.57) | copy-start | bytes 6148
  898.6 50.0 %copy-start.59 = (f32[768]{0:T(1024)S(1)}, f32[768]{0:T(1024)}, u32[]{:S(2)}) copy-start(f32[768]{0:T(1024)} %get-tuple-element.361) | copy-start | bytes 9220
  898.6 94.6 %copy-start.60 = (f32[512]{0:T(512)S(1)}, f32[512]{0:T(512)}, u32[]{:S(2)}) copy-start(f32[512]{0:T(512)} %get-tuple-element.479) | copy-start | bytes 6148
  944.1 49.2 %copy-start.28 = (f32[512,768]{1,0:T(8,128)S(1)}, f32[512,768]{1,0:T(8,128)}, u32[]{:S(2)}) copy-start(f32[512,768]{1,0:T(8,128)} %reduce-scatter.11.cloned.1.call-done) | copy-start | bytes 4718596
  1400.2 4.8 copy-start.1
  (24 other events, 54.2 us)
Sparse Core Ops, SparseCore 0:
  14.4 46.4 all-gather.4
  68.2 32.1 all-reduce.7
  192.2 71.2 reduce-scatter.4
  265.2 43.8 all-gather.8
  311.3 43.8 all-gather.6
  367.8 82.5 all-reduce.11
  477.2 71.2 reduce-scatter.8
  551.5 70.0 reduce-scatter.6
  625.9 43.8 all-gather.10
  874.0 70.0 reduce-scatter.10
  948.1 440.0 all-reduce.9
where the time goes:
time: 1420 us; the launch traced here: 1410 us
  waiting for transfers between devices  918 us (65%)
  matrix products  176 us (12%)
  local copies, waits for them, and re-layouts  161 us (11%)
  other arithmetic  69.4 us (5%)
  blocking collectives  66.8 us (5%)
  between operations  14.9 us (1%)
    psum x1, waiting for transfers between devices, on_device(): lax.psum((gw_down, gw_gateup, gw_in, gw_out), 'dp')  392 us
    reduce_scatter x4, waiting for transfers between devices, token_sum(): lax.psum_scatter(jnp.einsum('tj,jc->tc', source, weight, preferred_elemen...  247 us
    all_gather x4, waiting for transfers between devices, gather_tokens(): return lax.all_gather(values, 'row', axis=0, tiled=True)  165 us
    psum x2, waiting for transfers between devices, width_sum(): return lax.psum(values, 'col')  114 us
    dynamic_update_slice x16, local copies, waits for them, and re-layouts, attend_forward(): mixed, logsum = lax.map(one_block, (query_seq, jnp.arange(count)))  70.9 us
    psum x1, blocking collectives, on_device(): gain_a, gain_f = lax.psum((part_gain_attn, part_gain_ffn), ('dp', 'row'))  44.6 us
    dot_general x4, matrix products, token_sum(): jnp.einsum('tj,jc->tc', source, weight, preferred_element_type=jnp.float32)  31.1 us
  transfers between devices with their start and end apart: 11, of which 11 were waited for; matrix products, arithmetic and copies ran while one was open for 4% of the time, Pallas kernels for 0%

commit v1 on v0

--- a/solution.py
+++ b/solution.py
@@ -8,6 +8,19 @@
 LENGTH = 1024
 EPS = 1e-05
 THETA = 100000.0
+
+
+def ring_gather(array, axis, dim):
+    ways = lax.axis_size(axis)
+    up = [(d, (d + 1) % ways) for d in range(ways)]
+    down = [(d, (d - 1) % ways) for d in range(ways)]
+    earlier, later = ([array], [array])
+    for _ in range(ways // 2):
+        earlier.append(lax.ppermute(earlier[-1], axis, up))
+    for _ in range((ways - 1) // 2):
+        later.append(lax.ppermute(later[-1], axis, down))
+    line = jnp.concatenate([*earlier[::-1], *later[1:]], axis=dim)
+    return jnp.roll(line, (lax.axis_index(axis) - ways // 2) * array.shape[dim], axis=dim)
 
 
 def rotate(values, heads, inverse):
@@ -136,7 +149,7 @@
 
 
 def gather_tokens(values):
-    return lax.all_gather(values, "row", axis=0, tiled=True)
+    return ring_gather(values, "row", 0)
 
 
 def width_sum(values):

time: 1420 us -> 1520 us (1.070)
  other arithmetic: 69.4 us -> 147 us
  starting transfers between devices: 0.45 us -> 17.1 us
    all_gather x4 -> x0, waiting for transfers between devices: 165 us -> none  [gather_tokens(): return lax.all_gather(values, 'row', axis=0, tiled=True)]
    ppermute x0 -> x12, waiting for transfers between devices: none -> 157 us  [the longest x8 111 us: ring_gather(): earlier.append(lax.ppermute(earlier[-1], axis, up))]
    concatenate x0 -> x4, other arithmetic: none -> 79.4 us  [ring_gather(): jnp.roll(line, (lax.axis_index(axis) - ways // 2) * array.shape[dim], axi...]
    ppermute x0 -> x12, starting transfers between devices: none -> 16.8 us  [the longest x8 10.5 us: ring_gather(): earlier.append(lax.ppermute(earlier[-1], axis, up))]
  transfers between devices with their start and end apart: 11 -> 19, of which waited for: 11 -> 17; matrix products, arithmetic and copies ran while one was open for 4% -> 5% of each run, Pallas kernels for 0% -> 0%
where the time goes in v1:
time: 1520 us; the launch traced here: 1500 us
  waiting for transfers between devices  920 us (61%)
  local copies, waits for them, and re-layouts  165 us (11%)
  matrix products  165 us (11%)
  other arithmetic  147 us (10%)
  blocking collectives  66.9 us (4%)
  starting transfers between devices  17.1 us (1%)
    psum x1, waiting for transfers between devices, on_device(): lax.psum((gw_down, gw_gateup, gw_in, gw_out), 'dp')  392 us
    reduce_scatter x4, waiting for transfers between devices, token_sum(): lax.psum_scatter(jnp.einsum('tj,jc->tc', source, weight, preferred_elemen...  257 us
    psum x2, waiting for transfers between devices, width_sum(): return lax.psum(values, 'col')  114 us
    ppermute x8, waiting for transfers between devices, ring_gather(): earlier.append(lax.ppermute(earlier[-1], axis, up))  111 us
    concatenate x4, other arithmetic, ring_gather(): jnp.roll(line, (lax.axis_index(axis) - ways // 2) * array.shape[dim], axi...  79.4 us
    dynamic_update_slice x16, local copies, waits for them, and re-layouts, attend_forward(): mixed, logsum = lax.map(one_block, (query_seq, jnp.arange(count)))  70.8 us
    ppermute x4, waiting for transfers between devices, ring_gather(): later.append(lax.ppermute(later[-1], axis, down))  45.8 us
    psum x1, blocking collectives, on_device(): gain_a, gain_f = lax.psum((part_gain_attn, part_gain_ffn), ('dp', 'row'))  44.7 us
  transfers between devices with their start and end apart: 19, of which 17 were waited for; matrix products, arithmetic and copies ran while one was open for 5% of the time, Pallas kernels for 0%

profile of v1, /device:TPU:0, one launch (start us, length us, event | category | flops | bytes accessed | tf_op | source)
XLA Modules:
  0.0 1502.7 jit_solution(7602956636046206462)
XLA Ops:
  17.2 18.3 %collective-permute-done = bf16[512,768]{1,0:T(8,128)(2,1)S(1)} collective-permute-done((bf16[512,768]{1,0:T(8,128)(2,1)S(1)}, bf16[512,768]{1,0:T(8,128)(2,1)S(1)}, u32[]{:S(2)}, u32[]{:S(2)}) %collective-permute-start) | collective-permute-done | bytes 786464 | tf_op jit(solution)/shard_map/ppermute | solution.py:19
  39.8 13.2 collective-permute-done.2
  53.0 15.8 %collective-permute-done.1 = bf16[512,768]{1,0:T(8,128)(2,1)} collective-permute-done((bf16[512,768]{1,0:T(8,128)(2,1)S(1)}, bf16[512,768]{1,0:T(8,128)(2,1)}, u32[]{:S(2)}, u32[]{:S(2)}) %collective-permute-start.1) | collective-permute-done | bytes 786464 | tf_op jit(solution)/shard_map/ppermute | solution.py:19
  68.8 15.6 %fusion.120 = bf16[2048,768]{1,0:T(8,128)(2,1)S(1)} fusion(s32[]{:T(128)S(6)} %select_n.93, bf16[512,768]{1,0:T(8,128)(2,1)} %collective-permute-done.1, bf16[512,768]{1,0:T(8,128)(2,1)S(1)} %collective-permute-done, bf16[512,768]{1,0:T(8,128)(2,1)S(1)} %fusion.126, bf16[512,768]{1,0:T(8,128)(2,1)} %collective-permute-done.2), kind=kLoop, calls=%fused_computation.185 | loop fusion | flops 25165824 | bytes 6291460 | tf_op jit(solution)/shard_map/jit(_roll_dynamic)/concatenate | solution.py:23
  86.1 4.8 fusion.139
  92.4 31.3 %all-reduce.8.cloned.1.call-done = f32[2048,768]{1,0:T(8,128)} async-done(((f32[2048,768]{1,0:T(8,128)}), f32[2048,768]{1,0:T(8,128)}) %all-reduce.8.cloned.1.call-update) | async-done | bytes 6291472 | tf_op jit(solution)/shard_map/psum | solution.py:156
  129.8 3.8 slice.114
  133.5 3.5 copy.40
  149.7 25.8 %while.54 = (s32[]{:T(128)}, bf16[2,512,384]{2,1,0:T(8,128)(2,1)}, f32[2,2,2,512]{3,2,1,0:T(2,128)S(1)}, s32[2]{0:T(128)}, bf16[2,512,2,2,96]{1,4,3,2,0:T(8,128)...) while((s32[]{:T(128)}, bf16[2,512,384]{2,1,0:T(8,128)(2,1)}, ...), condition=%wide.region_6.8_spmd, body=%wide.region_3.7_spmd.sunk | while | flops 830994944 | bytes 30478976 | solution.py:84
  156.2 4.4 fusion.215
  169.1 4.4 fusion.215
  184.2 24.7 %while.55 = (s32[]{:T(128)}, bf16[2,512,384]{2,1,0:T(8,128)(2,1)}, f32[2,2,2,512]{3,2,1,0:T(2,128)}, s32[2]{0:T(128)}, bf16[2,512,2,2,96]{1,4,3,2,0:T(8,128)(2,1...) while((s32[]{:T(128)}, bf16[2,512,384]{2,1,0:T(8,128)(2,1)}, ...), condition=%wide.region_10.12_spmd, body=%wide.region_7.11_spmd.sunk | while | flops 830994944 | bytes 30610104 | solution.py:84
  191.1 3.6 fusion.218
  203.3 3.6 fusion.218
  208.9 6.6 fusion.134
  217.4 80.9 %reduce-scatter.5.cloned.1.call-done = f32[512,768]{1,0:T(8,128)} async-done(((f32[2048,768]{1,0:T(8,128)}), f32[512,768]{1,0:T(8,128)}) %reduce-scatter.5.cloned.1.call-update) | async-done | bytes 1572880 | tf_op jit(solution)/shard_map/reduce_scatter | solution.py:160
  309.1 15.1 %collective-permute-done.3 = bf16[512,768]{1,0:T(8,128)(2,1)S(1)} collective-permute-done((bf16[512,768]{1,0:T(8,128)(2,1)S(1)}, bf16[512,768]{1,0:T(8,128)(2,1)S(1)}, u32[]{:S(2)}, u32[]{:S(2)}) %collective-permute-start.3) | collective-permute-done | bytes 786464 | tf_op jit(solution)/shard_map/ppermute | solution.py:19
  324.8 16.3 %collective-permute-done.8 = bf16[512,768]{1,0:T(8,128)(2,1)S(1)} collective-permute-done((bf16[512,768]{1,0:T(8,128)(2,1)}, bf16[512,768]{1,0:T(8,128)(2,1)S(1)}, u32[]{:S(2)}, u32[]{:S(2)}) %collective-permute-start.8) | collective-permute-done | bytes 786464 | tf_op jit(solution)/shard_map/ppermute | solution.py:21
  341.1 16.8 %collective-permute-done.7 = bf16[512,768]{1,0:T(8,128)(2,1)S(1)} collective-permute-done((bf16[512,768]{1,0:T(8,128)(2,1)}, bf16[512,768]{1,0:T(8,128)(2,1)S(1)}, u32[]{:S(2)}, u32[]{:S(2)}) %collective-permute-start.7) | collective-permute-done | bytes 786464 | tf_op jit(solution)/shard_map/ppermute | solution.py:19
  357.9 16.0 %fusion.106 = bf16[2048,768]{1,0:T(8,128)(2,1)S(1)} fusion(s32[]{:T(128)S(6)} %select_n.93, bf16[512,768]{1,0:T(8,128)(2,1)S(1)} %collective-permute-done.7, bf16[512,768]{1,0:T(8,128)(2,1)} %collective-permute-done.6, bf16[512,768]{1,0:T(8,128)(2,1)} %param.31, bf16[512,768]{1,0:T(8,128)(2,1)S(1)} %collective-permute-done.8), kind=kLoop, calls=%fused_computation.171 | loop fusion | flops 25165824 | bytes 6291460 | tf_op jit(solution)/shard_map/jit(_roll_dynamic)/concatenate | solution.py:23
  374.0 5.9 fusion.158
  379.9 10.9 collective-permute-done.4
  390.8 28.9 %fusion.113 = bf16[2048,768]{1,0:T(8,128)(2,1)S(1)} fusion(s32[]{:T(128)S(6)} %select_n.93, bf16[512,768]{1,0:T(8,128)(2,1)S(1)} %collective-permute-done.4, bf16[512,768]{1,0:T(8,128)(2,1)S(1)} %collective-permute-done.3, bf16[512,768]{1,0:T(8,128)(2,1)S(1)} %multiply_convert_fusion.3, bf16[512,768]{1,0:T(8,128)(2,1)S(1)} %collective-permute-done.5), kind=kLoop, calls=%fused_computation.178 | loop fusion | flops 25165824 | bytes 6291460 | tf_op jit(solution)/shard_map/jit(_roll_dynamic)/concatenate | solution.py:23
  421.5 9.5 fusion.156
  431.1 82.7 %all-reduce.12.cloned.1.call-done = (f32[2048,2048]{1,0:T(8,128)}, f32[2048,1024]{1,0:T(8,128)}) async-done(((f32[2048,2048]{1,0:T(8,128)}, f32[2048,1024]{1,0:T(8,128)}), (f32[2048,2048]{1,0:T(8,128)}, f32[2048,1024]{1,0:T(8,128)})) %all-reduce.12.cloned.1.call-update) | async-done | bytes 25165840 | tf_op jit(solution)/shard_map/psum | solution.py:156
  513.8 13.3 multiply_convert_fusion.1
  530.3 8.6 fusion.95
  539.0 8.5 fusion.157
  547.6 62.8 %reduce-scatter.9.cloned.1.call-done = f32[512,768]{1,0:T(8,128)} async-done(((f32[2048,768]{1,0:T(8,128)}), f32[512,768]{1,0:T(8,128)}) %reduce-scatter.9.cloned.1.call-update) | async-done | bytes 1572880 | tf_op jit(solution)/shard_map/reduce_scatter | solution.py:160
  615.4 67.9 %reduce-scatter.7.cloned.1.call-done = f32[512,768]{1,0:T(8,128)} async-done(((f32[2048,768]{1,0:T(8,128)}), f32[512,768]{1,0:T(8,128)}) %reduce-scatter.7.cloned.1.call-update) | async-done | bytes 1572880 | tf_op jit(solution)/shard_map/reduce_scatter | solution.py:160
  683.3 4.1 fusion.151
  690.4 18.6 %collective-permute-done.9 = bf16[512,768]{1,0:T(8,128)(2,1)S(1)} collective-permute-done((bf16[512,768]{1,0:T(8,128)(2,1)}, bf16[512,768]{1,0:T(8,128)(2,1)S(1)}, u32[]{:S(2)}, u32[]{:S(2)}) %collective-permute-start.9) | collective-permute-done | bytes 786464 | tf_op jit(solution)/shard_map/ppermute | solution.py:19
  709.6 16.3 %collective-permute-done.11 = bf16[512,768]{1,0:T(8,128)(2,1)S(1)} collective-permute-done((bf16[512,768]{1,0:T(8,128)(2,1)}, bf16[512,768]{1,0:T(8,128)(2,1)S(1)}, u32[]{:S(2)}, u32[]{:S(2)}) %collective-permute-start.11) | collective-permute-done | bytes 786464 | tf_op jit(solution)/shard_map/ppermute | solution.py:21
  725.8 15.6 %collective-permute-done.10 = bf16[512,768]{1,0:T(8,128)(2,1)S(1)} collective-permute-done((bf16[512,768]{1,0:T(8,128)(2,1)S(1)}, bf16[512,768]{1,0:T(8,128)(2,1)S(1)}, u32[]{:S(2)}, u32[]{:S(2)}) %collective-permute-start.10) | collective-permute-done | bytes 786464 | tf_op jit(solution)/shard_map/ppermute | solution.py:19
  741.4 18.8 %fusion.99 = bf16[2048,768]{1,0:T(8,128)(2,1)S(1)} fusion(s32[]{:T(128)S(6)} %select_n.93, bf16[512,768]{1,0:T(8,128)(2,1)S(1)} %collective-permute-done.10, bf16[512,768]{1,0:T(8,128)(2,1)S(1)} %collective-permute-done.9, bf16[512,768]{1,0:T(8,128)(2,1)} %get-tuple-element.442, bf16[512,768]{1,0:T(8,128)(2,1)S(1)} %collective-permute-done.11), kind=kLoop, calls=%fused_computation.164 | loop fusion | flops 25165824 | bytes 6291460 | tf_op jit(solution)/shard_map/jit(_roll_dynamic)/concatenate | solution.py:23
  761.9 3.5 fusion.159
  765.4 12.2 all-reduce.13
  778.9 4.8 reshape.360
  787.7 74.6 %while.56 = (s32[]{:T(128)}, f32[1024,2,96]{0,2,1:T(8,128)}, f32[1024,2,96]{0,2,1:T(8,128)}, f32[2,512,384]{1,0,2:T(2,128)}, bf16[2,512,2,2,96]{1,4,3,2,0:T(8,12...) while((s32[]{:T(128)}, f32[1024,2,96]{0,2,1:T(8,128)}, ...), condition=%wide.region_23.25_spmd.clone, body=%wide.region_21.24_spmd.clone.sunk | while | flops 2046425600 | bytes 131526960 | solution.py:138
  791.0 4.5 fusion.228
  800.2 14.9 dynamic_update_slice.36
  815.1 4.0 fusion.230
  819.1 5.7 fusion.231
  828.0 4.5 fusion.228
  837.3 14.9 dynamic_update_slice.36
  852.2 4.2 fusion.230
  856.4 6.0 fusion.231
  866.3 4.7 reshape.361
  871.0 3.6 copy.54
  876.2 70.0 %while.57 = (s32[]{:T(128)}, f32[1024,2,96]{0,2,1:T(8,128)S(1)}, f32[1024,2,96]{0,2,1:T(8,128)}, f32[2,512,384]{1,0,2:T(2,128)}, bf16[2,512,2,2,96]{1,4,3,2,0:T(...) while((s32[]{:T(128)}, f32[1024,2,96]{0,2,1:T(8,128)S(1)}, ...), condition=%wide.region_26.28_spmd.clone, body=%wide.region_24.27_spmd.clone.sunk | while | flops 2046425600 | bytes 133099856 | solution.py:138
  887.2 14.9 dynamic_update_slice.37
  905.3 5.8 fusion.244
  922.1 14.9 dynamic_update_slice.37
  940.2 6.0 fusion.244
  946.2 3.7 concatenate.74
  958.7 5.5 fusion.137
  964.3 8.5 fusion.160
  972.9 9.1 fusion.94
  984.9 4.1 fusion.136
  989.0 45.4 %reduce-scatter.11.cloned.1.call-done = f32[512,768]{1,0:T(8,128)} async-done(((f32[2048,768]{1,0:T(8,128)}), f32[512,768]{1,0:T(8,128)}) %reduce-scatter.11.cloned.1.call-update) | async-done | bytes 1572880 | tf_op jit(solution)/shard_map/reduce_scatter | solution.py:160
  1039.1 44.7 %all-reduce = (f32[768]{0:T(1024)}, f32[768]{0:T(1024)}) all-reduce(f32[768]{0:T(1024)S(1)} %get-tuple-element.364, f32[768]{0:T(1024)S(1)} %copy-done.68), channel_id=1, replica_groups=mesh['dp'=4,'row'=4,'col'=2] {'dp','row'}, use_global_device_ids=true, to_apply=%region_31.33 | all-reduce | flops 1536 | bytes 12288 | tf_op jit(solution)/shard_map/psum | solution.py:241
  1086.7 391.8 %all-reduce.10.cloned.1.call-done = (f32[768,768]{1,0:T(8,128)}, f32[384,768]{1,0:T(8,128)}, f32[768,2048]{1,0:T(8,128)}, f32[1024,768]{1,0:T(8,128)}) async-done(((f32[768,768]{1,0:T(8,128)}, f32[384,768]{1,0:T(8,128)}, f32[768,2048]{1,0:T(8,128)}, f32[1024,768]{1,0:T(8,128)}), (f32[768,768]{1,0:T(8,128)}, f32[384,768]{1,0:T(8,128)}, f32[768,2048]{1,0:T(8,128)}, ...) | async-done | bytes 12976144 | tf_op jit(solution)/shard_map/psum | solution.py:235
  1481.8 6.7 fusion.152
  1491.7 3.8 copy.157
  (329 shorter events, 182.2 us)
Async XLA Ops:
  7.2 366.8 %copy-start = (bf16[1024,768]{1,0:T(8,128)(2,1)S(1)}, bf16[1024,768]{1,0:T(8,128)(2,1)}, u32[]{:S(2)}) copy-start(bf16[1024,768]{1,0:T(8,128)(2,1)} %param.30) | copy-start | bytes 4718596
  7.2 116.6 %all-reduce.8.cloned.1.call-start = ((), (), s32[]{:S(2)}) async-start(), calls=%async_computation.4 | async-start | bytes 12582912 | tf_op jit(solution)/shard_map/psum | solution.py:156
  11.9 23.6 %copy-start.66 = (f32[512]{0:T(512)}, f32[512]{0:T(512)S(1)}, u32[]{:S(2)}) copy-start(f32[512]{0:T(512)S(1)} %get-tuple-element.481) | copy-start | bytes 6148
  13.3 22.2 %collective-permute-start = (bf16[512,768]{1,0:T(8,128)(2,1)S(1)}, bf16[512,768]{1,0:T(8,128)(2,1)S(1)}, u32[]{:S(2)}, u32[]{:S(2)}) collective-permute-start(bf16[512,768]{1,0:T(8,128)(2,1)S(1)} %fusion.126), channel_id=1, source_target_pairs={{0,2},{2,4},{4,6},{6,0},{1,3},{3,5},{5,7},{7,1},{8,10},{10,12},{12... | collective-permute-start | bytes 2359304 | tf_op jit(solution)/shard_map/ppermute | solution.py:19
  16.2 36.8 %collective-permute-start.2 = (bf16[512,768]{1,0:T(8,128)(2,1)S(1)}, bf16[512,768]{1,0:T(8,128)(2,1)}, u32[]{:S(2)}, u32[]{:S(2)}) collective-permute-start(bf16[512,768]{1,0:T(8,128)(2,1)S(1)} %fusion.126), channel_id=1, source_target_pairs={{0,6},{2,0},{4,2},{6,4},{1,7},{3,1},{5,3},{7,5},{8,14},{10,8},{12,... | collective-permute-start | bytes 2359304 | tf_op jit(solution)/shard_map/ppermute | solution.py:21
  35.5 33.3 %collective-permute-start.1 = (bf16[512,768]{1,0:T(8,128)(2,1)S(1)}, bf16[512,768]{1,0:T(8,128)(2,1)}, u32[]{:S(2)}, u32[]{:S(2)}) collective-permute-start(bf16[512,768]{1,0:T(8,128)(2,1)S(1)} %collective-permute-done), channel_id=1, source_target_pairs={{0,2},{2,4},{4,6},{6,0},{1,3},{3,5},{5,7},{7,1},{8,10},{10,12},{12... | collective-permute-start | bytes 2359304 | tf_op jit(solution)/shard_map/ppermute | solution.py:19
  37.7 46.7 %copy-start.53 = (bf16[768,192]{1,0:T(8,128)(2,1)}, bf16[768,192]{1,0:T(8,128)(2,1)S(1)}, u32[]{:S(2)}) copy-start(bf16[768,192]{1,0:T(8,128)(2,1)S(1)} %copy.38) | copy-start | bytes 884740
  39.8 46.3 %copy-start.55 = (bf16[768,192]{1,0:T(8,128)(2,1)S(1)}, bf16[768,192]{1,0:T(8,128)(2,1)}, u32[]{:S(2)}) copy-start(bf16[768,192]{1,0:T(8,128)(2,1)} %copy.39) | copy-start | bytes 884740
  39.8 46.3 %copy-start.70 = (bf16[768,384]{1,0:T(8,128)(2,1)S(1)}, bf16[768,384]{1,0:T(8,128)(2,1)}, u32[]{:S(2)}) copy-start(bf16[768,384]{1,0:T(8,128)(2,1)} %param.24) | copy-start | bytes 1769476
  90.9 207.4 %reduce-scatter.5.cloned.1.call-start = ((), (), s32[]{:S(2)}) async-start(), calls=%async_computation.5 | async-start | bytes 7864320 | tf_op jit(solution)/shard_map/reduce_scatter | solution.py:160
  92.4 47.3 %copy-start.20 = (f32[2048,48]{0,1:T(8,128)}, f32[2048,48]{0,1:T(8,128)S(1)}, u32[]{:S(2)}) copy-start(f32[2048,48]{0,1:T(8,128)S(1)} %get-tuple-element.478) | copy-start | bytes 1179652
  92.4 47.3 %copy-start.22 = (f32[2048,48]{0,1:T(8,128)}, f32[2048,48]{0,1:T(8,128)S(1)}, u32[]{:S(2)}) copy-start(f32[2048,48]{0,1:T(8,128)S(1)} %get-tuple-element.479) | copy-start | bytes 1179652
  175.5 8.7 copy-start.8
  175.5 8.7 copy-start.59
  208.9 6.6 copy-start.6
  208.9 6.6 copy-start.10
  208.9 6.6 copy-start.16
  215.5 87.1 %copy-start.64 = (f32[768]{0:T(1024)S(1)}, f32[768]{0:T(1024)}, u32[]{:S(2)}) copy-start(f32[768]{0:T(1024)} %param.23) | copy-start | bytes 9220
  215.5 298.3 %all-reduce.12.cloned.1.call-start = ((), (), s32[]{:S(2)}) async-start(), calls=%async_computation.10 | async-start | bytes 50331648 | tf_op jit(solution)/shard_map/psum | solution.py:156
  215.6 90.2 %collective-permute-start.6 = (bf16[512,768]{1,0:T(8,128)(2,1)}, bf16[512,768]{1,0:T(8,128)(2,1)}, u32[]{:S(2)}, u32[]{:S(2)}) collective-permute-start(bf16[512,768]{1,0:T(8,128)(2,1)} %param.31), channel_id=1, source_target_pairs={{0,2},{2,4},{4,6},{6,0},{1,3},{3,5},{5,7},{7,1},{8,10},{10,12},{12... | collective-permute-start | bytes 2359304 | tf_op jit(solution)/shard_map/ppermute | solution.py:19
  302.9 21.4 %collective-permute-start.3 = (bf16[512,768]{1,0:T(8,128)(2,1)S(1)}, bf16[512,768]{1,0:T(8,128)(2,1)S(1)}, u32[]{:S(2)}, u32[]{:S(2)}) collective-permute-start(bf16[512,768]{1,0:T(8,128)(2,1)S(1)} %multiply_convert_fusion.3), channel_id=1, source_target_pairs={{0,2},{2,4},{4,6},{6,0},{1,3},{3,5},{5,7},{7,1},{8,10},{10,12},{12... | collective-permute-start | bytes 2359304 | tf_op jit(solution)/shard_map/ppermute | solution.py:19
  304.4 36.7 %collective-permute-start.8 = (bf16[512,768]{1,0:T(8,128)(2,1)}, bf16[512,768]{1,0:T(8,128)(2,1)S(1)}, u32[]{:S(2)}, u32[]{:S(2)}) collective-permute-start(bf16[512,768]{1,0:T(8,128)(2,1)} %param.31), channel_id=1, source_target_pairs={{0,6},{2,0},{4,2},{6,4},{1,7},{3,1},{5,3},{7,5},{8,14},{10,8},{12,... | collective-permute-start | bytes 2359304 | tf_op jit(solution)/shard_map/ppermute | solution.py:21
  305.8 52.1 %collective-permute-start.7 = (bf16[512,768]{1,0:T(8,128)(2,1)}, bf16[512,768]{1,0:T(8,128)(2,1)S(1)}, u32[]{:S(2)}, u32[]{:S(2)}) collective-permute-start(bf16[512,768]{1,0:T(8,128)(2,1)} %collective-permute-done.6), channel_id=1, source_target_pairs={{0,2},{2,4},{4,6},{6,0},{1,3},{3,5},{5,7},{7,1},{8,10},{10,12},{12... | collective-permute-start | bytes 2359304 | tf_op jit(solution)/shard_map/ppermute | solution.py:19
  306.7 113.0 %copy-start.48 = (bf16[768,2048]{1,0:T(8,128)(2,1)}, bf16[768,2048]{1,0:T(8,128)(2,1)S(1)}, u32[]{:S(2)}) copy-start(bf16[768,2048]{1,0:T(8,128)(2,1)S(1)} %constant_dynamic-update-slice_fusion.2) | copy-start | bytes 9437188
  306.8 73.2 %collective-permute-start.5 = (bf16[512,768]{1,0:T(8,128)(2,1)S(1)}, bf16[512,768]{1,0:T(8,128)(2,1)S(1)}, u32[]{:S(2)}, u32[]{:S(2)}) collective-permute-start(bf16[512,768]{1,0:T(8,128)(2,1)S(1)} %multiply_convert_fusion.3), channel_id=1, source_target_pairs={{0,6},{2,0},{4,2},{6,4},{1,7},{3,1},{5,3},{7,5},{8,14},{10,8},{12,... | collective-permute-start | bytes 2359304 | tf_op jit(solution)/shard_map/ppermute | solution.py:21
  324.2 66.6 %collective-permute-start.4 = (bf16[512,768]{1,0:T(8,128)(2,1)S(1)}, bf16[512,768]{1,0:T(8,128)(2,1)S(1)}, u32[]{:S(2)}, u32[]{:S(2)}) collective-permute-start(bf16[512,768]{1,0:T(8,128)(2,1)S(1)} %collective-permute-done.3), channel_id=1, source_target_pairs={{0,2},{2,4},{4,6},{6,0},{1,3},{3,5},{5,7},{7,1},{8,10},{10,12},{12... | collective-permute-start | bytes 2359304 | tf_op jit(solution)/shard_map/ppermute | solution.py:19
  374.0 5.9 copy-start.37
  431.0 179.4 %reduce-scatter.9.cloned.1.call-start = ((), (), s32[]{:S(2)}) async-start(), calls=%async_computation.7 | async-start | bytes 7864320 | tf_op jit(solution)/shard_map/reduce_scatter | solution.py:160
  513.8 16.5 %copy-start.49 = (bf16[768,2048]{1,0:T(8,128)(2,1)S(1)}, bf16[768,2048]{1,0:T(8,128)(2,1)}, u32[]{:S(2)}) copy-start(bf16[768,2048]{1,0:T(8,128)(2,1)} %copy-done.48) | copy-start | bytes 9437188
  538.9 144.4 %reduce-scatter.7.cloned.1.call-start = ((), (), s32[]{:S(2)}) async-start(), calls=%async_computation.6 | async-start | bytes 7864320 | tf_op jit(solution)/shard_map/reduce_scatter | solution.py:160
  547.5 486.9 %reduce-scatter.11.cloned.1.call-start = ((), (), s32[]{:S(2)}) async-start(), calls=%async_computation.8 | async-start | bytes 7864320 | tf_op jit(solution)/shard_map/reduce_scatter | solution.py:160
  610.4 72.9 %copy-start.29 = (f32[512,768]{1,0:T(8,128)S(1)}, f32[512,768]{1,0:T(8,128)}, u32[]{:S(2)}) copy-start(f32[512,768]{1,0:T(8,128)} %reduce-scatter.9.cloned.1.call-done) | copy-start | bytes 4718596
  687.5 21.5 %collective-permute-start.9 = (bf16[512,768]{1,0:T(8,128)(2,1)}, bf16[512,768]{1,0:T(8,128)(2,1)S(1)}, u32[]{:S(2)}, u32[]{:S(2)}) collective-permute-start(bf16[512,768]{1,0:T(8,128)(2,1)} %get-tuple-element.442), channel_id=1, source_target_pairs={{0,2},{2,4},{4,6},{6,0},{1,3},{3,5},{5,7},{7,1},{8,10},{10,12},{12... | collective-permute-start | bytes 2359304 | tf_op jit(solution)/shard_map/ppermute | solution.py:19
  688.9 36.9 %collective-permute-start.11 = (bf16[512,768]{1,0:T(8,128)(2,1)}, bf16[512,768]{1,0:T(8,128)(2,1)S(1)}, u32[]{:S(2)}, u32[]{:S(2)}) collective-permute-start(bf16[512,768]{1,0:T(8,128)(2,1)} %get-tuple-element.442), channel_id=1, source_target_pairs={{0,6},{2,0},{4,2},{6,4},{1,7},{3,1},{5,3},{7,5},{8,14},{10,8},{12,... | collective-permute-start | bytes 2359304 | tf_op jit(solution)/shard_map/ppermute | solution.py:21
  709.0 32.4 %collective-permute-start.10 = (bf16[512,768]{1,0:T(8,128)(2,1)S(1)}, bf16[512,768]{1,0:T(8,128)(2,1)S(1)}, u32[]{:S(2)}, u32[]{:S(2)}) collective-permute-start(bf16[512,768]{1,0:T(8,128)(2,1)S(1)} %collective-permute-done.9), channel_id=1, source_target_pairs={{0,2},{2,4},{4,6},{6,0},{1,3},{3,5},{5,7},{7,1},{8,10},{10,12},{12... | collective-permute-start | bytes 2359304 | tf_op jit(solution)/shard_map/ppermute | solution.py:19
  709.6 52.3 %copy-start.52 = (bf16[384,768]{1,0:T(8,128)(2,1)S(1)}, bf16[384,768]{1,0:T(8,128)(2,1)}, u32[]{:S(2)}) copy-start(bf16[384,768]{1,0:T(8,128)(2,1)} %param.27) | copy-start | bytes 1769476
  778.9 8.8 copy-start.9
  778.9 8.8 copy-start.13
  778.9 8.8 copy-start.60
  789.1 6.4 copy-start.2
  826.1 6.4 copy-start.2
  866.3 9.8 copy-start.7
  866.3 9.8 copy-start.11
  866.3 9.8 copy-start.17
  866.3 9.8 copy-start.63
  877.5 5.0 copy-start.3
  905.3 5.8 copy-start.18
  940.2 6.0 copy-start.18
  946.2 6.4 copy-start.21
  946.2 6.4 copy-start.23
  958.2 6.0 copy-start.50
  964.3 514.3 %all-reduce.10.cloned.1.call-start = ((), (), s32[]{:S(2)}) async-start(), calls=%async_computation.9 | async-start | bytes 25952256 | tf_op jit(solution)/shard_map/psum | solution.py:235
  964.3 8.5 copy-start.31
  964.3 8.5 copy-start.33
  964.3 8.5 copy-start.39
  972.8 9.1 copy-start.41
  972.8 9.1 copy-start.42
  972.8 9.1 copy-start.43
  989.0 45.5 %copy-start.15 = (bf16[512,768]{1,0:T(8,128)(2,1)S(1)}, bf16[512,768]{1,0:T(8,128)(2,1)}, u32[]{:S(2)}) copy-start(bf16[512,768]{1,0:T(8,128)(2,1)} %param.21) | copy-start | bytes 2359300
  989.0 45.5 %copy-start.65 = (f32[768]{0:T(1024)S(1)}, f32[768]{0:T(1024)}, u32[]{:S(2)}) copy-start(f32[768]{0:T(1024)} %param.22) | copy-start | bytes 9220
  989.0 45.5 %copy-start.67 = (f32[512]{0:T(512)S(1)}, f32[512]{0:T(512)}, u32[]{:S(2)}) copy-start(f32[512]{0:T(512)} %copy-done.66) | copy-start | bytes 6148
  989.0 50.1 %copy-start.68 = (f32[768]{0:T(1024)S(1)}, f32[768]{0:T(1024)}, u32[]{:S(2)}) copy-start(f32[768]{0:T(1024)} %get-tuple-element.362) | copy-start | bytes 9220
  989.0 94.7 %copy-start.69 = (f32[512]{0:T(512)S(1)}, f32[512]{0:T(512)}, u32[]{:S(2)}) copy-start(f32[512]{0:T(512)} %get-tuple-element.480) | copy-start | bytes 6148
  1034.5 49.2 %copy-start.28 = (f32[512,768]{1,0:T(8,128)S(1)}, f32[512,768]{1,0:T(8,128)}, u32[]{:S(2)}) copy-start(f32[512,768]{1,0:T(8,128)} %reduce-scatter.11.cloned.1.call-done) | copy-start | bytes 4718596
  (38 other events, 103.6 us)
Sparse Core Ops, SparseCore 0:
  91.0 32.7 all-reduce.7
  215.6 82.5 reduce-scatter.4
  431.2 82.6 all-reduce.11
  539.1 71.2 reduce-scatter.8
  613.2 70.0 reduce-scatter.6
  964.4 70.0 reduce-scatter.10
  1038.5 440.0 all-reduce.9
